TPU v7x, 32 devices: a whole 2x2x4 slice. The times are simulated.
32 devices in a mesh: expert: 4 (over y, core), shard: 8 (over z, x).
Axes of the slice: x: 2, y: 2, z: 4, core: 2. Of those that a mesh axis runs over, the one named last changes fastest.
Arguments:
- master_down: float32 [16, 6400, 4096], P('expert', None, 'shard'), may hold values from -0.109375 to 0.109375
- second_down: bfloat16 [16, 6400, 4096], P('expert', None, 'shard'), may hold values from -0.0390625 to 0.0390625
- router_weight: float32 [4096, 16], P('shard', 'expert'), may hold values from -0.09375 to 0.09375
- router_gain: float32 [4096], P('shard'), may hold values from 0.25 to 1.75
Outputs:
- final_down: bfloat16 [16, 6400, 4096], P('expert', 'shard')
- scale_down: float32 [16, 6400], P('expert', 'shard')
- serve_router: bfloat16 [4096, 16], replicated
All inputs are finite; a program needn't handle non-finite values.
Results may differ from a plain program's by a relative error of at most 0.0085.
Values may be sent and summed in bfloat16 or wider, within the bound.
A program may use at most 256 MiB of HBM per device.

v0:
```python
import jax
import jax.numpy as jnp
from jax import lax
from jax.sharding import PartitionSpec as P


def body(master_down, second_down, router_weight, router_gain):
    merged_down = master_down + second_down.astype(jnp.float32)
    total_down = lax.psum(
        jnp.sum(merged_down * merged_down, axis=2).astype(jnp.bfloat16), "shard"
    ).astype(jnp.float32)
    scale_down = jnp.sqrt(total_down)
    narrow_down = (merged_down / jnp.expand_dims(scale_down, 2)).astype(jnp.bfloat16)
    final_down = lax.all_to_all(narrow_down, "shard", split_axis=1, concat_axis=2, tiled=True)
    scale_down = lax.dynamic_slice_in_dim(
        scale_down, lax.axis_index("shard") * final_down.shape[1], final_down.shape[1], axis=1
    )
    part_router = (router_weight * router_gain[:, None]).astype(jnp.bfloat16)
    row_router = lax.all_gather(part_router, "shard", axis=0, tiled=True)
    serve_router = lax.all_gather(row_router, "expert", axis=1, tiled=True)
    return (final_down, scale_down, serve_router)


def solution(mesh):
    placed = (
        P("expert", None, "shard"),
        P("expert", None, "shard"),
        P("shard", "expert"),
        P("shard"),
    )
    return jax.shard_map(
        body,
        mesh=mesh,
        in_specs=placed,
        out_specs=(P("expert", "shard", None), P("expert", "shard"), P()),
        check_vma=False,
    )
```

profile of v0, /device:TPU:11, one launch (start us, length us, event | category | flops | bytes accessed | tf_op | source)
XLA Modules:
  0.0 823.1 jit_solution(7862156734528137198)
XLA Ops:
  0.6 24.2 %multiply_reduce_fusion = bf16[4,6400]{1,0:T(4,128)(2,1)S(1)} fusion(f32[4,6400,512]{2,1,0:T(8,128)} %param.4, bf16[4,6400,512]{2,1,0:T(8,128)(2,1)} %param.5), kind=kLoop, calls=%fused_computation.1 | loop fusion | flops 52403200 | bytes 78694400 | tf_op jit(solution)/shard_map/reduce_sum | solution.py:10
  24.9 0.9 copy.21
  25.8 71.1 %psum.7 = bf16[4,6400]{0,1:T(8,128)(2,1)} all-reduce(bf16[4,6400]{0,1:T(8,128)(2,1)S(1)} %copy.21), channel_id=1, replica_groups=mesh['expert'=4,'shard'=8] {'shard'}, use_global_device_ids=true, to_apply=%region_1.0 | all-reduce | flops 25600 | bytes 102400 | tf_op jit(solution)/shard_map/psum | solution.py:9
  96.9 2.3 convert_sqrt_fusion
  99.2 1.2 copy.17
  100.4 34.3 %divide_convert_fusion = bf16[4,6400,512]{2,1,0:T(8,128)(2,1)} fusion(f32[4,6400,512]{2,1,0:T(8,128)} %param.4, bf16[4,6400,512]{2,1,0:T(8,128)(2,1)} %param.5, f32[4,6400]{1,0:T(4,128)S(1)} %copy.17), kind=kLoop, calls=%fused_computation | loop fusion | flops 52428800 | bytes 104960000 | tf_op jit(solution)/shard_map/convert_element_type | solution.py:13
  134.7 33.4 %copy.18 = bf16[4,6400,512]{2,0,1:T(4,128)(2,1)} copy(bf16[4,6400,512]{2,1,0:T(8,128)(2,1)} %divide_convert_fusion) | data formatting | bytes 52428800 | tf_op jit(solution)/shard_map/convert_element_type | solution.py:13
  168.1 0.0 copy-start
  168.1 0.0 copy-start.1
  168.1 8.5 %all-to-all-start = ((bf16[4,6400,512]{2,0,1:T(4,128)(2,1)}), bf16[4,6400,512]{2,0,1:T(4,128)(2,1)}, u32[]{:S(2)}, u32[]{:S(2)}) async-start(bf16[4,6400,512]{2,0,1:T(4,128)(2,1)} %copy.18), calls=%async_computation | async-start | bytes 52428800 | tf_op jit(solution)/shard_map/all_to_all | solution.py:14
  176.6 0.8 constant_dynamic-slice_fusion
  177.3 1.8 copy.20
  179.1 0.0 copy-done
  179.1 0.0 copy-done.1
  179.1 573.2 %all_gather.6 = bf16[4096,4]{0,1:T(4,128)(2,1)S(1)} all-gather(bf16[512,4]{0,1:T(4,128)(2,1)S(1)} %multiply_convert_fusion), channel_id=1, replica_groups=mesh['expert'=4,'shard'=8] {'shard'}, dimensions={0}, use_global_device_ids=true | all-gather | bytes 36864 | tf_op jit(solution)/shard_map/all_gather | solution.py:19
  752.3 12.7 %all-gather = bf16[4,4,4096]{2,1,0:T(4,128)(2,1)S(1)} all-gather(bf16[1,4,4096]{2,1,0:T(4,128)(2,1)S(1)} %bitcast.9), channel_id=1, replica_groups=mesh['expert'=4,'shard'=8] {'expert'}, dimensions={0}, use_global_device_ids=true | all-gather | bytes 163840 | tf_op jit(solution)/shard_map/all_gather | solution.py:20
  765.0 0.7 reshape.9
  765.7 0.0 all-to-all-done
  765.7 18.2 %copy.19 = bf16[4,800,8,512]{3,2,1,0:T(8,128)(2,1)} copy(bf16[4,800,8,512]{3,0,1,2:T(4,128)(2,1)} %bitcast.1) | data formatting | bytes 52428800 | tf_op jit(solution)/shard_map/all_to_all | solution.py:14
  783.9 39.2 %all_to_all.16 = bf16[4,800,4096]{2,1,0:T(8,128)(2,1)} reshape(bf16[4,800,8,512]{3,2,1,0:T(8,128)(2,1)} %copy.19) | data formatting | bytes 52428800 | tf_op jit(solution)/shard_map/all_to_all | solution.py:14
  (1 shorter events, 0.0 us)
Async XLA Ops:
  168.1 11.1 %copy-start = (f32[512,4]{0,1:T(4,128)S(1)}, f32[512,4]{0,1:T(4,128)}, u32[]{:S(2)}) copy-start(f32[512,4]{0,1:T(4,128)} %param.6) | copy-start | bytes 24580
  168.1 11.1 %copy-start.1 = (f32[512]{0:T(512)S(1)}, f32[512]{0:T(512)}, u32[]{:S(2)}) copy-start(f32[512]{0:T(512)} %param.7) | copy-start | bytes 6148
  168.1 597.6 %all-to-all-start = ((bf16[4,6400,512]{2,0,1:T(4,128)(2,1)}), bf16[4,6400,512]{2,0,1:T(4,128)(2,1)}, u32[]{:S(2)}, u32[]{:S(2)}) async-start(bf16[4,6400,512]{2,0,1:T(4,128)(2,1)} %copy.18), calls=%async_computation | async-start | bytes 52428800 | tf_op jit(solution)/shard_map/all_to_all | solution.py:14
where the time goes:
time: 828 us; the launch traced here: 823 us
  blocking collectives  657 us (79%)
  local copies, waits for them, and re-layouts  96.2 us (12%)
  other arithmetic  60.8 us (7%)
  starting transfers between devices  8.5 us (1%)
    all_gather x1, blocking collectives, body(): row_router = lax.all_gather(part_router, 'shard', axis=0, tiled=True)  573 us
    psum x1, blocking collectives, body(): lax.psum(jnp.sum(merged_down * merged_down, axis=2).astype(jnp.bfloat16),...  71.1 us
    all_to_all x2, local copies, waits for them, and re-layouts, body(): lax.all_to_all(narrow_down, 'shard', split_axis=1, concat_axis=2, tiled=T...  57.4 us
    convert_element_type x1, other arithmetic, body(): (merged_down / jnp.expand_dims(scale_down, 2)).astype(jnp.bfloat16)  34.3 us
    convert_element_type x1, local copies, waits for them, and re-layouts, body(): (merged_down / jnp.expand_dims(scale_down, 2)).astype(jnp.bfloat16)  33.4 us
    reduce_sum x1, other arithmetic, body(): jnp.sum(merged_down * merged_down, axis=2).astype(jnp.bfloat16)  24.2 us
  transfers between devices with their start and end apart: 1, of which 0 were waited for; matrix products, arithmetic and copies ran while one was open for 0% of the time, Pallas kernels for 0%

commit v1 on v0

v1 whole, which is shorter than its diff:
```python
import functools

import jax
import jax.numpy as jnp
from jax import lax
from jax.experimental import pallas as pl
from jax.experimental.pallas import tpu as pltpu
from jax.sharding import PartitionSpec as P

ANY = pl.BlockSpec(memory_space=pl.ANY)
MESH = pl.DeviceIdType.MESH


def rows_of(rows, most):
    best = [r for r in range(8, min(rows, most) + 1, 8) if rows % r == 0]
    return best[-1] if best else rows


def merge(master_ref, second_ref, out_ref):
    out_ref[...] = (master_ref[...] + second_ref[...].astype(jnp.float32)).astype(out_ref.dtype)


def exchange(shards, experts, held, order, step_rows, master, second, router, got, staged, routers,
             send_sem, recv_sem, rsend_sem, rrecv_sem, esend_sem, erecv_sem, own_sem):
    me = lax.axis_index("shard")
    mine = lax.axis_index("expert")
    rows, columns = got.shape[2:]

    barrier = pltpu.get_barrier_semaphore()

    def greet_shard(k, carry):
        pl.semaphore_signal(barrier, inc=1, device_id={"shard": lax.rem(me + k, shards)}, device_id_type=MESH)
        return carry

    def greet_expert(k, carry):
        pl.semaphore_signal(barrier, inc=1, device_id={"expert": lax.rem(mine + k, experts)}, device_id_type=MESH)
        return carry

    lax.fori_loop(1, shards, greet_shard, 0)
    lax.fori_loop(1, experts, greet_expert, 0)
    pl.semaphore_wait(barrier, shards + experts - 2)

    def router_rows(to, origin):
        return pltpu.make_async_remote_copy(
            src_ref=router, dst_ref=routers.at[mine, me], send_sem=rsend_sem.at[to], recv_sem=rrecv_sem.at[origin],
            device_id={"shard": to}, device_id_type=MESH)

    def router_columns(to, origin):
        return pltpu.make_async_remote_copy(
            src_ref=routers.at[mine], dst_ref=routers.at[mine], send_sem=esend_sem.at[to], recv_sem=erecv_sem.at[origin],
            device_id={"expert": to}, device_id_type=MESH)

    def block(to, origin, e):
        return pltpu.make_async_remote_copy(
            src_ref=staged.at[to, e], dst_ref=got.at[me, e], send_sem=send_sem.at[to, e], recv_sem=recv_sem.at[origin, e],
            device_id={"shard": to}, device_id_type=MESH)

    own_router = pltpu.make_async_copy(router, routers.at[mine, me], own_sem)
    own_router.start()

    def start_rows(k, carry):
        router_rows(lax.rem(me + k, shards), me).start()
        return carry

    lax.fori_loop(1, shards, start_rows, 0)

    spec = pl.BlockSpec((step_rows, columns), lambda i: (i, 0))
    merged = pltpu.emit_pipeline(merge, grid=(rows // step_rows,), in_specs=[spec, spec], out_specs=[spec])

    def send_block(i, carry):
        e, k = i // (shards - 1), lax.rem(i, shards - 1)
        to = lax.rem(me + order(k, mine, e), shards)
        merged(master.at[e, to], second.at[e, to], staged.at[to, e])
        block(to, me, e).start()
        return carry

    lax.fori_loop(0, held * (shards - 1), send_block, 0)

    def wait_rows(k, carry):
        peer = lax.rem(me + k, shards)
        router_rows(peer, peer).wait()
        return carry

    own_router.wait()
    lax.fori_loop(1, shards, wait_rows, 0)

    def start_columns(k, carry):
        router_columns(lax.rem(mine + k, experts), mine).start()
        return carry

    lax.fori_loop(1, experts, start_columns, 0)

    def own_block(e, carry):
        merged(master.at[e, me], second.at[e, me], got.at[me, e])
        return carry

    lax.fori_loop(0, held, own_block, 0)

    def wait_columns(k, carry):
        peer = lax.rem(mine + k, experts)
        router_columns(peer, peer).wait()
        return carry

    lax.fori_loop(1, experts, wait_columns, 0)

    def wait_block(i, carry):
        e, k = i // (shards - 1), lax.rem(i, shards - 1)
        peer = lax.rem(me + 1 + k, shards)
        block(peer, peer, e).wait()
        return carry

    lax.fori_loop(0, held * (shards - 1), wait_block, 0)


def normalise(got_ref, out_ref, scale_ref):
    shards, _, rows, columns = got_ref.shape
    total = jnp.zeros((rows, columns), jnp.float32)
    for s in range(shards):
        part = got_ref[s, 0].astype(jnp.float32)
        total = total + part * part
    scale = jnp.sqrt(jnp.sum(total, axis=1, keepdims=True))
    scale_ref[0] = scale
    inverse = 1.0 / scale
    for s in range(shards):
        out_ref[0, :, s * columns:(s + 1) * columns] = (
            got_ref[s, 0].astype(jnp.float32) * inverse).astype(out_ref.dtype)


def in_turn(shards, k, mine, e):
    return 1 + k


def make(mesh, order=None, most=160, norm_rows=160):
    shards, experts = mesh.shape["shard"], mesh.shape["expert"]
    order = functools.partial(in_turn if order is None else order, shards)

    def body(master_down, second_down, router_weight, router_gain):
        held, wide, columns = master_down.shape
        rows = wide // shards
        router = (router_weight * router_gain[:, None]).astype(jnp.bfloat16).T
        step_rows = rows_of(rows, most)
        got, _, routers = pl.pallas_call(
            functools.partial(exchange, shards, experts, held, order, step_rows),
            out_shape=[
                jax.ShapeDtypeStruct((shards, held, rows, columns), jnp.bfloat16),
                jax.ShapeDtypeStruct((shards, held, rows, columns), jnp.bfloat16),
                jax.ShapeDtypeStruct((experts, shards) + router.shape, jnp.bfloat16),
            ],
            in_specs=[ANY] * 3,
            out_specs=[ANY] * 3,
            scratch_shapes=[
                pltpu.SemaphoreType.DMA((shards, held)),
                pltpu.SemaphoreType.DMA((shards, held)),
                pltpu.SemaphoreType.DMA((shards,)),
                pltpu.SemaphoreType.DMA((shards,)),
                pltpu.SemaphoreType.DMA((experts,)),
                pltpu.SemaphoreType.DMA((experts,)),
                pltpu.SemaphoreType.DMA,
            ],
            compiler_params=pltpu.CompilerParams(collective_id=0, has_side_effects=True),
            name="exchange",
        )(
            master_down.reshape(held, shards, rows, columns),
            second_down.reshape(held, shards, rows, columns),
            router,
        )
        norm = rows_of(rows, norm_rows)
        final_down, scale_down = pl.pallas_call(
            normalise,
            grid=(held, rows // norm),
            in_specs=[pl.BlockSpec((shards, 1, norm, columns), lambda e, i: (0, e, i, 0))],
            out_specs=[
                pl.BlockSpec((1, norm, shards * columns), lambda e, i: (e, i, 0)),
                pl.BlockSpec((1, norm, 1), lambda e, i: (e, i, 0)),
            ],
            out_shape=[
                jax.ShapeDtypeStruct((held, rows, shards * columns), jnp.bfloat16),
                jax.ShapeDtypeStruct((held, rows, 1), jnp.float32),
            ],
            name="normalise",
        )(got)
        serve_router = routers.transpose(1, 3, 0, 2).reshape(shards * router.shape[1], experts * router.shape[0])
        return final_down, scale_down[:, :, 0], serve_router

    placed = (P("expert", None, "shard"), P("expert", None, "shard"), P("shard", "expert"), P("shard"))
    return jax.shard_map(
        body,
        mesh=mesh,
        in_specs=placed,
        out_specs=(P("expert", "shard", None), P("expert", "shard"), P()),
        check_vma=False,
    )


def solution(mesh):
    return make(mesh)
```

time: 828 us -> 615 us (0.74)
  blocking collectives: 657 us -> 0 us
  Pallas kernels: 0 us -> 605 us
  local copies, waits for them, and re-layouts: 96.2 us -> 1.63 us
  other arithmetic: 60.8 us -> 3.88 us
  starting transfers between devices: 8.5 us -> 0 us
    pallas_call x0 -> x2, Pallas kernels: none -> 605 us  [the longest x1 576 us: body(): pl.pallas_call(functools.partial(exchange, shards, experts, held, order,...]
    all_gather x2 -> x0, blocking collectives: 586 us -> none  [the longest x1 573 us: body(): row_router = lax.all_gather(part_router, 'shard', axis=0, tiled=True)]
    psum x1 -> x0, blocking collectives: 71.1 us -> none  [body(): lax.psum(jnp.sum(merged_down * merged_down, axis=2).astype(jnp.bfloat16),...]
    all_to_all x2 -> x0, local copies, waits for them, and re-layouts: 57.4 us -> none  [body(): lax.all_to_all(narrow_down, 'shard', split_axis=1, concat_axis=2, tiled=T...]
    convert_element_type x2 -> x0, other arithmetic: 34.3 us -> none  [the longest x1 34.3 us: body(): (merged_down / jnp.expand_dims(scale_down, 2)).astype(jnp.bfloat16)]
    convert_element_type x1 -> x0, local copies, waits for them, and re-layouts: 33.4 us -> none  [body(): (merged_down / jnp.expand_dims(scale_down, 2)).astype(jnp.bfloat16)]
    reduce_sum x1 -> x0, other arithmetic: 24.2 us -> none  [body(): jnp.sum(merged_down * merged_down, axis=2).astype(jnp.bfloat16)]
    all_to_all x1 -> x0, starting transfers between devices: 8.5 us -> none  [body(): lax.all_to_all(narrow_down, 'shard', split_axis=1, concat_axis=2, tiled=T...]
  transfers between devices with their start and end apart: 1 -> 0, of which waited for: 0 -> 0; matrix products, arithmetic and copies ran while one was open for 0% -> 0% of each run, Pallas kernels for 0% -> 0%
where the time goes in v1:
time: 615 us; the launch traced here: 612 us
  Pallas kernels  605 us (98%)
    pallas_call x1, Pallas kernels, body(): pl.pallas_call(functools.partial(exchange, shards, experts, held, order,...  576 us
    pallas_call x1, Pallas kernels, body(): pl.pallas_call(normalise, grid=(held, rows // norm), in_specs=[pl.BlockSp...  29 us

profile of v1, /device:TPU:11, one launch (start us, length us, event | category | flops | bytes accessed | tf_op | source)
XLA Modules:
  0.0 611.6 jit_solution(12754059841012017334)
XLA Ops:
  0.6 1.3 fusion.router
  1.9 576.5 %exchange.1 = (bf16[8,4,800,512]{3,2,1,0:T(8,128)(2,1)}, bf16[8,4,800,512]{3,2,1,0:T(8,128)(2,1)}, bf16[4,8,4,512]{3,2,1,0:T(4,128)(2,1)}) custom-call(f32[4,8,800,512]{3,2,1,0:T(8,128)} %bitcast.10, bf16[4,8,800,512]{3,2,1,0:T(8,128)(2,1)} %bitcast.11, bf16[4,512]{1,0:T(4,128)(2,1)} %fusion.router), custom_call_target="tpu_custom_call" | custom-call | tf_op jit(solution)/shard_map/exchange/pallas_call | solution.py:142
  578.4 0.9 copy.7
  579.4 0.7 copy.8
  580.0 29.0 %normalise.1 = (bf16[4,800,4096]{2,1,0:T(8,128)(2,1)}, f32[4,800,1]{2,1,0:T(8,128)}) custom-call(bf16[8,4,800,512]{3,2,1,0:T(8,128)(2,1)} %get-tuple-element.7.got_ref), custom_call_target="tpu_custom_call" | custom-call | tf_op jit(solution)/shard_map/normalise/pallas_call | solution.py:168
  609.1 2.6 reduce
